TPU v7x, 256 devices: a whole 4x4x8 slice. The times are simulated.
256 devices in a mesh: grp: 8 (over y, core), ep: 32 (over x, z).
Axes of the slice: x: 4, y: 4, z: 8, core: 2. Of those that a mesh axis runs over, the one named last changes fastest.
Arguments:
- d_out: bfloat16 [32768, 2048], P(('grp', 'ep')), may hold values from -12 to 12
- routes: int32 [32768, 2], P(('grp', 'ep')), may hold values from 0 to 7, all different within a row; in each aligned block of 128 rows (0 to 127, 128 to 255, ...) at most 48 rows name the same one
- combine: float32 [32768, 2], P(('grp', 'ep')), may hold values from 0.05 to 1
- live_tokens: int32 [256], P(('grp', 'ep')), may hold values from 1 to 128, as said below
- hidden: bfloat16 [12288, 57344], P('grp', 'ep'), may hold values from -6 to 6
Outputs:
- expert_grad: float32 [2048, 57344], P('grp', 'ep')
Inputs may be any that keep to these rules, and one draw needn't show every extreme that they name: `routes`: the two experts of a token differ. Among the 128 rows of one device no expert is named by more than 48 rows, and on some devices one expert is named by exactly 48 rows. `live_tokens`: the live tokens of a device are its first ones; on the last device all 128 are live.
All inputs are finite; a program needn't handle non-finite values.
Results may differ from a plain program's by a relative error of at most 0.0029.
Values may be sent and summed in bfloat16 or wider, within the bound.
A program may use at most 128 MiB of HBM per device.

v0:
```python
import jax
import jax.numpy as jnp
from jax import lax
from jax.sharding import Mesh
from jax.sharding import PartitionSpec as P

EXPERTS = 8
CAP = 48
EP = ("ep_0", "ep_1")
GRP_EP = ("grp_0", "grp_1", "ep_0", "ep_1")
GRP = ("grp_0", "grp_1")


def over_axes(x, axes):
    for axis in axes:
        x = lax.psum(x, axis)
    return x


def device_slots(d_rows, route_rows, weight_rows, live_count):
    tokens_here = d_rows.shape[0]
    alive = (jnp.arange(tokens_here, dtype=jnp.int32) < live_count).astype(jnp.float32)
    scaled = weight_rows * alive[:, None]
    weighted = (d_rows.astype(jnp.float32)[:, None, :] * scaled[:, :, None]).astype(jnp.bfloat16)
    weighted = weighted.reshape(tokens_here * route_rows.shape[1], d_rows.shape[1])
    flat = route_rows.reshape(-1)
    chosen = (flat[:, None] == jnp.arange(EXPERTS, dtype=jnp.int32)[None, :]).astype(jnp.int32)
    before = jnp.cumsum(chosen, axis=0, dtype=jnp.int32) - chosen
    position = jnp.sum(before * chosen, axis=1, dtype=jnp.int32)
    slot_index = flat * CAP + position
    placing = (jnp.arange(EXPERTS * CAP, dtype=jnp.int32)[:, None] == slot_index[None, :]).astype(
        jnp.bfloat16
    )
    buffer = jnp.dot(placing, weighted, preferred_element_type=jnp.float32).astype(jnp.bfloat16)
    alive_pairs = jnp.repeat(alive, route_rows.shape[1])
    counts = jnp.sum(chosen.astype(jnp.float32) * alive_pairs[:, None], axis=0)
    return (buffer.reshape(EXPERTS, CAP, d_rows.shape[1]), counts)


def on_device(d_out, routes, combine, live_tokens, hidden):
    width = d_out.shape[1]
    shards = lax.axis_size(EP) // EXPERTS
    my_expert = lax.axis_index(EP) // shards
    buffer, counts = device_slots(d_out, routes, combine, live_tokens[0])
    sending = jnp.repeat(buffer, shards, axis=0)
    arrived = lax.all_to_all(sending, EP, split_axis=0, concat_axis=0, tiled=True)
    totals = over_axes(counts, GRP_EP)
    picked = (jnp.arange(EXPERTS, dtype=jnp.int32) == my_expert).astype(jnp.float32)
    count = jnp.sum(totals * picked)
    slots = arrived.reshape(-1, width)
    total = lax.psum_scatter(
        lax.dot_general(
            slots, hidden, (((0,), (0,)), ((), ())), preferred_element_type=jnp.float32
        ),
        GRP,
        scatter_dimension=0,
        tiled=True,
    )
    return total * lax.rsqrt(1.0 + count)


def solution(mesh):
    finer = Mesh(mesh.devices.reshape(4, 2, 4, 8), ("grp_0", "grp_1", "ep_0", "ep_1"))
    placed = (P(GRP_EP, None), P(GRP_EP, None), P(GRP_EP, None), P(GRP_EP), P(GRP, EP))
    return jax.shard_map(
        on_device, mesh=finer, in_specs=placed, out_specs=P(GRP, EP), check_vma=False
    )
```

profile of v0, /device:TPU:2, one launch (start us, length us, event | category | flops | bytes accessed | tf_op | source)
XLA Modules:
  0.0 276.7 jit_solution(10427977377997912067)
XLA Ops:
  6.5 0.0 reduce-scatter.2.cloned.1.call-start
  6.5 0.8 copy.6
  7.3 0.1 reshape.49
  7.5 0.1 eq.46
  8.3 0.7 broadcast_multiply_fusion.1
  9.0 0.1 copy.8
  9.1 0.1 mul.68
  9.2 0.6 reduce-window.6
  9.8 0.2 slice_reduce_fusion
  10.1 0.1 fusion.3
  10.2 2.1 mul.64
  12.3 2.5 mul.65
  14.8 2.2 convolution_convert_fusion
  17.0 0.0 slice-start
  17.0 0.8 broadcast_in_dim.2
  17.8 0.0 slice-start.1
  17.9 150.1 %all_to_all.5 = bf16[32,48,2048]{2,1,0:T(8,128)(2,1)S(1)} all-to-all(bf16[32,48,2048]{2,1,0:T(8,128)(2,1)S(1)} %bitcast.11), channel_id=1, replica_groups=mesh['grp_0'=4,'grp_1'=2,'ep_0'=4,'ep_1'=8] {'ep_0','ep_1'}, dimensions={0} | all-to-all | bytes 12582912 | tf_op jit(solution)/shard_map/all_to_all | solution.py:46
  168.0 0.0 slice-done
  168.0 0.0 slice-done.1
  168.0 15.0 %fusion.8 = f32[2048,1792]{1,0:T(8,128)} fusion(bf16[1536,2048]{1,0:T(8,128)(2,1)S(1)} %bitcast.12, bf16[1536,1792]{1,0:T(8,128)(2,1)S(1)} %bitcast.15), kind=kOutput, calls=%fused_computation.21 | convolution fusion | flops 11274289152 | bytes 26476544 | tf_op jit(solution)/shard_map/dot_general | solution.py:52
  183.0 0.0 reduce-scatter.2.cloned.1.call-update
  183.0 0.1 mul.66.clone
  183.1 0.1 mul.72
  183.2 0.1 fusion.5
  183.3 10.7 %psum.28 = f32[8]{0:T(128)S(1)} all-reduce(f32[8]{0:T(128)S(1)} %fusion.5), channel_id=1, replica_groups=mesh['grp_0'=4,'grp_1'=2,'ep_0'=4,'ep_1'=8] {'grp_0'}, use_global_device_ids=true, to_apply=%region_5.6 | all-reduce | flops 8 | bytes 64 | tf_op jit(solution)/shard_map/psum | solution.py:16
  194.1 2.5 psum.29
  196.5 10.5 %psum.30 = f32[8]{0:T(128)S(1)} all-reduce(f32[8]{0:T(128)S(1)} %psum.29), channel_id=1, replica_groups=mesh['grp_0'=4,'grp_1'=2,'ep_0'=4,'ep_1'=8] {'ep_0'}, use_global_device_ids=true, to_apply=%region_7.8 | all-reduce | flops 8 | bytes 64 | tf_op jit(solution)/shard_map/psum | solution.py:16
  207.0 15.8 %psum.31 = f32[8]{0:T(128)S(1)} all-reduce(f32[8]{0:T(128)S(1)} %psum.30), channel_id=1, replica_groups=mesh['grp_0'=4,'grp_1'=2,'ep_0'=4,'ep_1'=8] {'ep_1'}, use_global_device_ids=true, to_apply=%region_8.9 | all-reduce | flops 8 | bytes 64 | tf_op jit(solution)/shard_map/psum | solution.py:16
  222.8 0.6 fusion.7
  224.1 42.9 %reduce-scatter.2.cloned.1.call-done = f32[256,1792]{1,0:T(8,128)} async-done(((f32[2048,1792]{1,0:T(8,128)}), f32[256,1792]{1,0:T(8,128)}) %reduce-scatter.2.cloned.1.call-update) | async-done | bytes 1835024 | tf_op jit(solution)/shard_map/reduce_scatter | solution.py:51
  267.0 2.8 %broadcast_multiply_fusion = f32[256,1792]{1,0:T(8,128)} fusion(f32[256,1792]{1,0:T(8,128)} %reduce-scatter.2.cloned.1.call-done, f32[]{:T(128)S(6)} %rsqrt.3), kind=kLoop, calls=%fused_computation.3 | loop fusion | flops 458752 | bytes 3670020 | tf_op jit(solution)/shard_map/mul | solution.py:59
  (6 shorter events, 0.1 us)
Async XLA Ops:
  6.5 260.5 %reduce-scatter.2.cloned.1.call-start = ((), (), s32[]{:S(2)}) async-start(), calls=%async_computation.2 | async-start | bytes 16515072 | tf_op jit(solution)/shard_map/reduce_scatter | solution.py:51
  17.0 151.0 %slice-start = ((s8[5505024]{0:T(1024)(128)(4,1)}), s8[4194304]{0:T(1024)(128)(4,1)S(1)}, s32[]{:S(2)}) async-start(s8[5505024]{0:T(1024)(128)(4,1)} %bitcast.14), calls=%async_computation.3 | async-start | bytes 8388608
  17.8 150.2 %slice-start.1 = ((s8[5505024]{0:T(1024)(128)(4,1)}), s8[1310720]{0:T(1024)(128)(4,1)S(1)}, s32[]{:S(2)}) async-start(s8[5505024]{0:T(1024)(128)(4,1)} %bitcast.14), calls=%async_computation.4 | async-start | bytes 2621440
Sparse Core Ops, SparseCore 0:
  183.1 83.8 reduce-scatter.1
where the time goes:
time: 277 us
  blocking collectives  190 us (69%)
  waiting for transfers between devices  43 us (16%)
  matrix products  17.2 us (6%)
  between operations  14.8 us (5%)
  local copies, waits for them, and re-layouts  7.16 us (3%)
  other arithmetic  4.98 us (2%)
    all_to_all x1, blocking collectives, on_device(): lax.all_to_all(sending, EP, split_axis=0, concat_axis=0, tiled=True)  150 us
    reduce_scatter x1, waiting for transfers between devices, on_device(): lax.psum_scatter(lax.dot_general(slots, hidden, (((0,), (0,)), ((), ())),...  42.9 us
    psum x4, blocking collectives, over_axes(): x = lax.psum(x, axis)  39.5 us
    dot_general x1, matrix products, on_device(): lax.dot_general(slots, hidden, (((0,), (0,)), ((), ())), preferred_elemen...  15 us
  transfers between devices with their start and end apart: 1, of which 1 were waited for; matrix products, arithmetic and copies ran while one was open for 0% of the time, Pallas kernels for 0%

commit v1 on v0

v1 whole, which is shorter than its diff:
```python
import functools

import jax
import jax.numpy as jnp
from jax import lax
from jax.experimental import pallas as pl
from jax.experimental.pallas import tpu as pltpu
from jax.sharding import PartitionSpec as P

EXPERTS = 8
CAP = 48
TOK = 128
CHUNKS = 4
WIDE = 256
HALF = 128
BF = jnp.bfloat16
F32 = jnp.float32


def rcopy(src, dst, ssem, rsem, dev):
    return pltpu.make_async_remote_copy(
        src_ref=src, dst_ref=dst, send_sem=ssem, recv_sem=rsem, device_id=dev,
        device_id_type=pl.DeviceIdType.MESH,
    )


def kernel(
    d_ref, routes_ref, comb_ref, live_ref, hid_ref, out_ref,
    Z, R, S, TR, HB, PB, SC, M, CN, RT, ACC, YS, YV,
    lsem, psem, prx, hsem, hps, hrx, mps, mrx, zs, zx, ms, mx,
    xs, rx, tx, fs, ys, yx, cs, cx,
):
    g = lax.axis_index("grp")
    e = lax.axis_index("ep")
    y, c = g // 2, g % 2
    x, z = e // 8, e % 8
    h = z // 4
    oc = 1 - c

    mate = (y * 2 + oc, e)
    zp = (g, x * 8 + (z + 1) % 8)
    zm = (g, x * 8 + (z + 7) % 8)
    xp = (g, ((x + 1) % 4) * 8 + z)
    xm = (g, ((x + 3) % 4) * 8 + z)
    yp = (((y + 1) % 4) * 2 + c, e)
    ym = (((y + 3) % 4) * 2 + c, e)
    bx1 = (g, (x + 1 - 2 * (x % 2)) * 8 + z)
    bx2 = (g, (3 - x) * 8 + z)
    by1 = ((y + 1 - 2 * (y % 2)) * 2 + c, e)
    by2 = ((3 - y) * 2 + c, e)

    barrier = pltpu.get_barrier_semaphore()
    for dev in (mate, zp, zm, xp, xm, yp, ym):
        pl.semaphore_signal(barrier, inc=1, device_id=dev, device_id_type=pl.DeviceIdType.MESH)

    def column(i, half, core):
        dest = ((y + 2) % 4, None, None, y)[i]
        if dest is None:
            dest = (y + 1) % 4 if half == 0 else (y + 3) % 4
            off = 0 if i == 1 else HALF
        else:
            off = half * HALF
        return pl.ds(pl.multiple_of(WIDE * (2 * dest + core) + off, HALF), HALF)

    mine = pl.ds(pl.multiple_of(c * TOK, TOK), TOK)
    his = pl.ds(pl.multiple_of(oc * TOK, TOK), TOK)

    for i in range(CHUNKS):
        for half in range(2):
            pltpu.make_async_copy(
                d_ref.at[:, column(i, half, c)],
                Z.at[i, z, mine, pl.ds(half * HALF, HALF)],
                lsem.at[i],
            ).start()
    own_rows = pl.ds(pl.multiple_of(c * 1536, 256), 1536)
    mate_rows = pl.ds(pl.multiple_of(oc * 1536, 256), 1536)
    pltpu.make_async_copy(hid_ref, HB.at[own_rows], hsem).start()

    er = lax.broadcasted_iota(jnp.int32, (EXPERTS, TOK), 0)
    tok = lax.broadcasted_iota(jnp.int32, (EXPERTS, TOK), 1)
    first = routes_ref[0:1, :] == er
    second = routes_ref[1:2, :] == er
    chosen = jnp.where(first, 1.0, 0.0) + jnp.where(second, 1.0, 0.0)
    before = (
        lax.broadcasted_iota(jnp.int32, (TOK, TOK), 0)
        < lax.broadcasted_iota(jnp.int32, (TOK, TOK), 1)
    )
    position = jnp.dot(
        chosen.astype(BF), jnp.where(before, 1.0, 0.0).astype(BF), preferred_element_type=F32
    )
    alive = jnp.where(tok < live_ref[0], chosen, 0.0)
    M[z, c, 0:8, :] = jnp.where(alive > 0.0, position, -1.0)
    M[z, c, 8:16, :] = jnp.where(first, comb_ref[0:1, :], 0.0) + jnp.where(
        second, comb_ref[1:2, :], 0.0
    )

    pl.semaphore_wait(barrier, 7)

    rcopy(M.at[z, c], M.at[z, c], mps, mrx, mate).start()
    for i in range(CHUNKS):
        for half in range(2):
            rcopy(
                d_ref.at[:, column(i, half, oc)],
                Z.at[i, z, mine, pl.ds(half * HALF, HALF)],
                psem, prx.at[i], mate,
            ).start()
    hid_copy = rcopy(hid_ref, HB.at[own_rows], hps, hrx, mate)
    hid_copy.start()

    slot_iota = lax.broadcasted_iota(jnp.int32, (CAP, TOK), 0).astype(F32)

    def rows_of(xx, zz):
        return pl.ds(pl.multiple_of((xx * 8 + zz) * CAP, 16), CAP)

    def build_p(b, zz):
        for cc in range(2):
            for k in range(4):
                ex = 2 * ((x + k) % 4) + h
                hit = slot_iota == M[zz, cc, pl.ds(ex, 1), :]
                weight = jnp.where(hit, M[zz, cc, pl.ds(8 + ex, 1), :], 0.0)
                PB[b, cc, CAP * k:CAP * (k + 1), :] = jnp.where(hit, 1.0, 0.0).astype(BF)
                SC[b, cc, CAP * k:CAP * (k + 1), :] = jnp.broadcast_to(
                    jnp.sum(weight, axis=1, keepdims=True), (CAP, TOK)
                )

    def process(i, b, zz):
        @pl.when(i == 0)
        def _():
            build_p(b, zz)

        own = rows_of(x, zz)
        for cc in range(2):
            picked = jnp.dot(
                PB[b, cc], Z[i, zz, cc * TOK:(cc + 1) * TOK, :], preferred_element_type=F32
            )
            scale = SC[b, cc]
            slots = (picked * jnp.concatenate([scale, scale], axis=1)).astype(BF)
            R[i, cc, own, :] = slots[0:CAP]
            for k in range(1, 4):
                S[i, b, k - 1, cc] = slots[CAP * k:CAP * (k + 1)]
        rcopy(S.at[i, b, 0], R.at[i, :, own, :], xs, rx.at[i, 0], xp).start()
        rcopy(S.at[i, b, 2], R.at[i, :, own, :], xs, rx.at[i, 1], xm).start()
        rcopy(S.at[i, b, 1, 0], TR.at[i, b, 0], xs, tx.at[i, b, 0], xp).start()
        rcopy(S.at[i, b, 1, 1], TR.at[i, b, 1], xs, tx.at[i, b, 1], xm).start()

    def forward(i, b, zz):
        for side, dev, src in ((0, xp, (x + 3) % 4), (1, xm, (x + 1) % 4)):
            rcopy(TR.at[i, b, side], TR.at[i, b, side], fs, tx.at[i, b, side], dev).wait_recv()
            rcopy(
                TR.at[i, b, side], R.at[i, side, rows_of(src, zz), :], fs, rx.at[i, 2 + side], dev
            ).start()

    def zsend(i, zz, side, hop, whole):
        dev = (zp, zm)[side]
        ref = Z.at[i, zz] if whole else Z.at[i, zz, pl.ds(side * TOK, TOK)]
        rcopy(ref, ref, zs, zx.at[i, side, hop - 1], dev).start()

    def zwait(i, zz, side, hop, whole):
        dev = (zp, zm)[side]
        ref = Z.at[i, zz] if whole else Z.at[i, zz, pl.ds(side * TOK, TOK)]
        rcopy(ref, ref, zs, zx.at[i, side, hop - 1], dev).wait_recv()

    def msend(zz, side, hop, whole):
        dev = (zp, zm)[side]
        ref = M.at[zz] if whole else M.at[zz, side]
        rcopy(ref, ref, ms, mx.at[side, hop - 1], dev).start()

    def mwait(zz, side, hop, whole):
        dev = (zp, zm)[side]
        ref = M.at[zz] if whole else M.at[zz, side]
        rcopy(ref, ref, ms, mx.at[side, hop - 1], dev).wait_recv()

    def away(hop, side):
        return (z + 8 - hop) % 8 if side == 0 else (z + hop) % 8

    def unit0(i):
        pltpu.make_async_copy(Z.at[i, z, mine], Z.at[i, z, mine], lsem.at[i]).wait()
        rcopy(Z.at[i, z, his], Z.at[i, z, his], psem, prx.at[i], mate).wait_recv()
        for side in range(2):
            zsend(i, z, side, 1, True)
        process(i, 0, z)

    def unit(i, hop):
        for side in range(2):
            block = away(hop, side)

            @pl.when(i == 0)
            def _():
                mwait(block, side, hop, True)
                msend(block, side, hop + 1, hop < 3)

            zwait(i, block, side, hop, True)
            zsend(i, block, side, hop + 1, hop < 3)
        process(i, 2 * hop - 1, away(hop, 0))
        process(i, 2 * hop, away(hop, 1))

    def unit4(i):
        block = away(4, 1)

        @pl.when(i == 0)
        def _():
            for side in range(2):
                mwait(block, side, 4, False)

        for side in range(2):
            zwait(i, block, side, 4, False)
        process(i, 7, block)

    def forward_unit(i, hop):
        if hop == 0:
            forward(i, 0, z)
        elif hop == 4:
            forward(i, 7, away(4, 1))
        else:
            forward(i, 2 * hop - 1, away(hop, 0))
            forward(i, 2 * hop, away(hop, 1))

    def multiply(ch):
        for n in range(2):
            dev = (xp, xm)[n]
            whole = R.at[ch, :, pl.ds(0, 8 * CAP), :]
            rcopy(whole, whole, xs, rx.at[ch, n], dev).wait_recv()
            part = R.at[ch, n, pl.ds(0, 8 * CAP), :]
            rcopy(part, part, fs, rx.at[ch, 2 + n], dev).wait_recv()

        for cc in range(2):
            @pl.loop(0, 6)
            def _(k):
                rows = pl.ds(pl.multiple_of(k * 256, 256), 256)
                cols = pl.ds(pl.multiple_of(cc * 1536 + k * 256, 256), 256)
                RT[:, cols] = R[ch, cc, rows, :].T

        @pl.loop(0, 7)
        def _(n):
            cols = pl.ds(pl.multiple_of(n * 256, 256), 256)
            ACC[:, cols] = jnp.dot(RT[...], HB[:, cols], preferred_element_type=F32)

    def ywait(ch, half):
        ref = YV.at[ch, half]
        rcopy(ref, ref, ys, yx.at[ch, half], (yp, ym)[half]).wait_recv()

    def reduce_send(ch):
        for half in range(2):
            @pl.when(ch == half + 1)
            def _():
                ywait(0, half)

                @pl.loop(0, 7)
                def _(n):
                    cols = pl.ds(pl.multiple_of(n * 256, 256), 256)
                    ACC[half * HALF:(half + 1) * HALF, cols] += YV[0, half, :, cols].astype(F32)

            @pl.loop(0, 7)
            def _(n):
                cols = pl.ds(pl.multiple_of(n * 256, 256), 256)
                YS[ch, half, :, cols] = ACC[half * HALF:(half + 1) * HALF, cols].astype(BF)

            rcopy(YS.at[ch, half], YV.at[ch, half], ys, yx.at[ch, half], (yp, ym)[half]).start()

    def count_send(step):
        dev = (bx1, bx2, by1, by2)[step]
        rcopy(CN.at[0, step], CN.at[1, step], cs, cx.at[step], dev).start()

    def count_wait(step):
        dev = (bx1, bx2, by1, by2)[step]
        rcopy(CN.at[1, step], CN.at[1, step], cs, cx.at[step], dev).wait_recv()
        return CN[0, step] + CN[1, step]

    rcopy(M.at[z, oc], M.at[z, oc], mps, mrx, mate).wait_recv()
    for side in range(2):
        msend(z, side, 1, True)
    unit0(0)

    @pl.loop(0, 5)
    def _(q):
        later = jnp.maximum(q - 1, 0)

        @pl.when(q >= 1)
        def _():
            unit4(later)

        @pl.when(q < 4)
        def _():
            unit(q, 1)
            forward_unit(q, 0)

        @pl.when(q >= 1)
        def _():
            forward_unit(later, 4)

        @pl.when(q == 1)
        def _():
            total = jnp.zeros((EXPERTS, TOK), F32)
            for zz in range(8):
                for cc in range(2):
                    total += jnp.where(M[zz, cc, 0:8, :] >= 0.0, 1.0, 0.0)
            CN[0, 0] = total
            count_send(0)

        for step in range(3):
            @pl.when(q == step + 2)
            def _():
                CN[0, step + 1] = count_wait(step)
                count_send(step + 1)

        @pl.when(q < 4)
        def _():
            unit(q, 2)
            forward_unit(q, 1)
            unit(q, 3)

        @pl.when(q < 3)
        def _():
            unit0(q + 1)

        @pl.when(q < 4)
        def _():
            forward_unit(q, 2)

        @pl.when(q == 1)
        def _():
            pltpu.make_async_copy(hid_ref, HB.at[own_rows], hsem).wait()
            rcopy(hid_ref, HB.at[mate_rows], hps, hrx, mate).wait_recv()

        @pl.when((q >= 1) & (q < 4))
        def _():
            multiply(later)
            reduce_send(later)

        @pl.when(q < 4)
        def _():
            forward_unit(q, 3)

    multiply(3)
    total = count_wait(3)
    picked = jnp.where(er == 2 * x + h, total, 0.0)
    count = jnp.sum(jnp.sum(picked, axis=1, keepdims=True), axis=0, keepdims=True)
    factor = lax.rsqrt(1.0 + count)
    for ch in (1, 2):
        for half in range(2):
            ywait(ch, half)
    for part in range(2):
        rows = slice(part * HALF, (part + 1) * HALF)

        @pl.loop(0, 7)
        def _(n):
            cols = pl.ds(pl.multiple_of(n * 256, 256), 256)
            out_ref[rows, cols] = (
                ACC[rows, cols]
                + YV[part + 1, 0, :, cols].astype(F32)
                + YV[part + 1, 1, :, cols].astype(F32)
            ) * factor

    rcopy(M.at[z, c], M.at[z, c], mps, mrx, mate).wait_send()
    sent = Z.at[:, 0, pl.ds(0, TOK)]
    rcopy(sent, sent, psem, prx.at[0], mate).wait_send()
    hid_copy.wait_send()
    sent = M.at[pl.ds(0, 7)]
    rcopy(sent, sent, ms, mx.at[0, 0], zp).wait_send()
    sent = Z.at[:, pl.ds(0, 7)]
    rcopy(sent, sent, zs, zx.at[0, 0, 0], zp).wait_send()
    rcopy(S, S, xs, rx.at[0, 0], xp).wait_send()
    rcopy(TR, TR, fs, rx.at[0, 0], xp).wait_send()
    rcopy(YS, YS, ys, yx.at[0, 0], yp).wait_send()
    rcopy(CN.at[0], CN.at[0], cs, cx.at[0], bx1).wait_send()


def on_device(d_out, routes, combine, live_tokens, hidden):
    dma = pltpu.SemaphoreType.DMA
    any_spec = pl.BlockSpec(memory_space=pl.ANY)
    vmem = pl.BlockSpec(memory_space=pltpu.VMEM)
    return pl.pallas_call(
        kernel,
        out_shape=jax.ShapeDtypeStruct((WIDE, 1792), F32),
        in_specs=[any_spec, vmem, vmem, pl.BlockSpec(memory_space=pltpu.SMEM), any_spec],
        out_specs=vmem,
        scratch_shapes=[
            pltpu.VMEM((CHUNKS, 8, 2 * TOK, WIDE), BF),
            pltpu.VMEM((CHUNKS, 2, 32 * CAP, WIDE), BF),
            pltpu.VMEM((CHUNKS, 8, 3, 2, CAP, WIDE), BF),
            pltpu.VMEM((CHUNKS, 8, 2, CAP, WIDE), BF),
            pltpu.VMEM((2 * 1536, 1792), BF),
            pltpu.VMEM((8, 2, 4 * CAP, TOK), BF),
            pltpu.VMEM((8, 2, 4 * CAP, TOK), F32),
            pltpu.VMEM((8, 2, 16, TOK), F32),
            pltpu.VMEM((2, 4, EXPERTS, TOK), F32),
            pltpu.VMEM((WIDE, 2 * 1536), BF),
            pltpu.VMEM((WIDE, 1792), F32),
            pltpu.VMEM((3, 2, HALF, 1792), BF),
            pltpu.VMEM((3, 2, HALF, 1792), BF),
            dma((CHUNKS,)), dma, dma((CHUNKS,)), dma, dma, dma, dma, dma,
            dma, dma((CHUNKS, 2, 4)), dma, dma((2, 4)),
            dma, dma((CHUNKS, 4)), dma((CHUNKS, 8, 2)), dma,
            dma, dma((3, 2)), dma, dma((4,)),
        ],
        compiler_params=pltpu.CompilerParams(
            collective_id=0, has_side_effects=True, vmem_limit_bytes=64000000
        ),
    )(d_out, routes.T, combine.T, live_tokens, hidden)


def solution(mesh):
    both = P(("grp", "ep"), None)
    return jax.shard_map(
        on_device, mesh=mesh,
        in_specs=(both, both, both, P(("grp", "ep")), P("grp", "ep")),
        out_specs=P("grp", "ep"), check_vma=False,
    )
```

time: 277 us -> 105 us (0.38)
  blocking collectives: 190 us -> 0 us
  Pallas kernels: 0 us -> 102 us
  waiting for transfers between devices: 43 us -> 0 us
  matrix products: 17.2 us -> 0 us
  between operations: 14.8 us -> 0.66 us
  other arithmetic: 4.98 us -> 0 us
  local copies, waits for them, and re-layouts: 7.16 us -> 2.85 us
    all_to_all x1 -> x0, blocking collectives: 150 us -> none  [on_device(): lax.all_to_all(sending, EP, split_axis=0, concat_axis=0, tiled=True)]
    pallas_call x0 -> x1, Pallas kernels: none -> 102 us  [on_device(): pl.pallas_call(kernel, out_shape=jax.ShapeDtypeStruct((WIDE, 1792), F32),...]
    reduce_scatter x1 -> x0, waiting for transfers between devices: 42.9 us -> none  [on_device(): lax.psum_scatter(lax.dot_general(slots, hidden, (((0,), (0,)), ((), ())),...]
    psum x4 -> x0, blocking collectives: 39.5 us -> none  [over_axes(): x = lax.psum(x, axis)]
    dot_general x2 -> x0, matrix products: 17.2 us -> none  [the longest x1 15 us: on_device(): lax.dot_general(slots, hidden, (((0,), (0,)), ((), ())), preferred_elemen...]
    mul x6 -> x0, local copies, waits for them, and re-layouts: 5.07 us -> none  [the longest x3 4.73 us: device_slots(): d_rows.astype(jnp.float32)[:, None, :] * scaled[:, :, None]]
    mul x2 -> x0, other arithmetic: 3.53 us -> none  [the longest x1 2.85 us: on_device(): return total * lax.rsqrt(1.0 + count)]
  transfers between devices with their start and end apart: 1 -> 0, of which waited for: 1 -> 0; matrix products, arithmetic and copies ran while one was open for 0% -> 0% of each run, Pallas kernels for 0% -> 0%
where the time goes in v1:
time: 105 us
  Pallas kernels  102 us (97%)
  local copies, waits for them, and re-layouts  2.85 us (3%)
    pallas_call x1, Pallas kernels, on_device(): pl.pallas_call(kernel, out_shape=jax.ShapeDtypeStruct((WIDE, 1792), F32),...  102 us
    unnamed x1, local copies, waits for them, and re-layouts  2.85 us

profile of v1, /device:TPU:2, one launch (start us, length us, event | category | flops | bytes accessed | tf_op | source)
XLA Modules:
  0.0 105.3 jit_solution(387295797605976682)
XLA Ops:
  0.7 101.8 %shard_map.55 = f32[256,1792]{1,0:T(8,128)} custom-call(bf16[128,2048]{1,0:T(8,128)(2,1)} %d_ref.1, s32[2,128]{1,0:T(2,128)} %bitcast.2, f32[2,128]{1,0:T(2,128)} %bitcast.3, s32[1]{0:T(128)S(6)} %copy.7.live_ref, bf16[1536,1792]{1,0:T(8,128)(2,1)} %hid_ref.1), custom_call_target="tpu_custom_call" | custom-call | tf_op jit(solution)/shard_map/pallas_call | solution.py:372
  102.5 2.8 %copy.8 = f32[256,1792]{1,0:T(8,128)} copy(f32[256,1792]{1,0:T(8,128)} %shard_map.55) | data formatting | bytes 3670016

commit v2 on v1

v2 whole, which is shorter than its diff:
```python
import functools

import jax
import jax.numpy as jnp
from jax import lax
from jax.experimental import pallas as pl
from jax.experimental.pallas import tpu as pltpu
from jax.sharding import PartitionSpec as P

EXPERTS = 8
CAP = 48
TOK = 128
CHUNKS = 4
WIDE = 256
HALF = 128
KB = 8 * CAP
BF = jnp.bfloat16
F32 = jnp.float32


def rcopy(src, dst, ssem, rsem, dev):
    return pltpu.make_async_remote_copy(
        src_ref=src, dst_ref=dst, send_sem=ssem, recv_sem=rsem, device_id=dev,
        device_id_type=pl.DeviceIdType.MESH,
    )


def kernel(
    d_ref, routes_ref, comb_ref, live_ref, hid_ref, out_ref,
    Z, R, S, HB, PB, SC, M, CN, RT, ACC, YS, YV,
    lsem, psem, prx, hsem, hps, hrx, mps, mrx, zs, zx, ms, mx,
    xs, rx, ys, yx, cs, cx,
):
    g = lax.axis_index("grp")
    e = lax.axis_index("ep")
    y, c = g // 2, g % 2
    x, z = e // 8, e % 8
    h = z // 4
    oc = 1 - c

    mate = (y * 2 + oc, e)
    zp = (g, x * 8 + (z + 1) % 8)
    zm = (g, x * 8 + (z + 7) % 8)
    xp = (g, ((x + 1) % 4) * 8 + z)
    xm = (g, ((x + 3) % 4) * 8 + z)
    xo = (g, ((x + 2) % 4) * 8 + z)
    yp = (((y + 1) % 4) * 2 + c, e)
    ym = (((y + 3) % 4) * 2 + c, e)
    bx1 = (g, (x + 1 - 2 * (x % 2)) * 8 + z)
    bx2 = (g, (3 - x) * 8 + z)
    by1 = ((y + 1 - 2 * (y % 2)) * 2 + c, e)
    by2 = ((3 - y) * 2 + c, e)

    barrier = pltpu.get_barrier_semaphore()
    for dev in (mate, zp, zm, xp, xm, xo, yp, ym):
        pl.semaphore_signal(barrier, inc=1, device_id=dev, device_id_type=pl.DeviceIdType.MESH)

    def column(i, half, core):
        dest = ((y + 2) % 4, None, None, y)[i]
        if dest is None:
            dest = (y + 1) % 4 if half == 0 else (y + 3) % 4
            off = 0 if i == 1 else HALF
        else:
            off = half * HALF
        return pl.ds(pl.multiple_of(WIDE * (2 * dest + core) + off, HALF), HALF)

    mine = pl.ds(pl.multiple_of(c * TOK, TOK), TOK)
    his = pl.ds(pl.multiple_of(oc * TOK, TOK), TOK)

    def source(b):
        hop = (b + 1) // 2
        return (z + 8 - hop) % 8 if b % 2 else (z + hop) % 8

    for i in range(CHUNKS):
        for half in range(2):
            pltpu.make_async_copy(
                d_ref.at[:, column(i, half, c)],
                Z.at[i, z, mine, pl.ds(half * HALF, HALF)],
                lsem.at[i],
            ).start()
    for b in range(8):
        pltpu.make_async_copy(hid_ref.at[:, source(b)], HB.at[b, c], hsem).start()

    er = lax.broadcasted_iota(jnp.int32, (EXPERTS, TOK), 0)
    tok = lax.broadcasted_iota(jnp.int32, (EXPERTS, TOK), 1)
    first = routes_ref[0:1, :] == er
    second = routes_ref[1:2, :] == er
    chosen = jnp.where(first, 1.0, 0.0) + jnp.where(second, 1.0, 0.0)
    before = (
        lax.broadcasted_iota(jnp.int32, (TOK, TOK), 0)
        < lax.broadcasted_iota(jnp.int32, (TOK, TOK), 1)
    )
    position = jnp.dot(
        chosen.astype(BF), jnp.where(before, 1.0, 0.0).astype(BF), preferred_element_type=F32
    )
    alive = jnp.where(tok < live_ref[...], chosen, 0.0)
    M[z, c, 0:8, :] = jnp.where(alive > 0.0, position, -1.0)
    M[z, c, 8:16, :] = jnp.where(first, comb_ref[0:1, :], 0.0) + jnp.where(
        second, comb_ref[1:2, :], 0.0
    )

    pl.semaphore_wait(barrier, 8)

    rcopy(M.at[z, c], M.at[z, c], mps, mrx, mate).start()
    for i in range(CHUNKS):
        for half in range(2):
            rcopy(
                d_ref.at[:, column(i, half, oc)],
                Z.at[i, z, mine, pl.ds(half * HALF, HALF)],
                psem, prx.at[i], mate,
            ).start()
    for b in range(8):
        rcopy(hid_ref.at[:, source(b)], HB.at[b, c], hps, hrx, mate).start()

    slot_iota = lax.broadcasted_iota(jnp.int32, (CAP, TOK), 0).astype(F32)

    def build_p(b, zz):
        for cc in range(2):
            for k in range(4):
                ex = 2 * ((x + k) % 4) + h
                hit = slot_iota == M[zz, cc, pl.ds(ex, 1), :]
                weight = jnp.where(hit, M[zz, cc, pl.ds(8 + ex, 1), :], 0.0)
                PB[b, cc, CAP * k:CAP * (k + 1), :] = jnp.where(hit, 1.0, 0.0).astype(BF)
                SC[b, cc, CAP * k:CAP * (k + 1), :] = jnp.broadcast_to(
                    jnp.sum(weight, axis=1, keepdims=True), (CAP, TOK)
                )

    def wave(b):
        return 0 if b < 5 else 1 if b < 7 else 2

    def process(*units):
        for i, b, zz in units:
            @pl.when(i == 0)
            def _():
                build_p(b, zz)

        for i, b, zz in units:
            for cc in range(2):
                picked = jnp.dot(
                    PB[b, cc], Z[i, zz, cc * TOK:(cc + 1) * TOK, :], preferred_element_type=F32
                )
                scale = SC[b, cc]
                slots = (picked * jnp.concatenate([scale, scale], axis=1)).astype(BF)
                R[i, b, cc, x] = slots[0:CAP]
                for k in range(1, 4):
                    S[i, b, k - 1, cc] = slots[CAP * k:CAP * (k + 1)]
        for i, b, zz in units:
            for k, dev in ((1, xo), (0, xp), (2, xm)):
                rcopy(S.at[i, b, k], R.at[i, b, :, x], xs, rx.at[i, k, wave(b)], dev).start()

    def zsend(i, zz, side, hop, whole):
        dev = (zp, zm)[side]
        ref = Z.at[i, zz] if whole else Z.at[i, zz, pl.ds(side * TOK, TOK)]
        rcopy(ref, ref, zs, zx.at[i, side, hop - 1], dev).start()

    def zwait(i, zz, side, hop, whole):
        dev = (zp, zm)[side]
        ref = Z.at[i, zz] if whole else Z.at[i, zz, pl.ds(side * TOK, TOK)]
        rcopy(ref, ref, zs, zx.at[i, side, hop - 1], dev).wait_recv()

    def msend(zz, side, hop, whole):
        dev = (zp, zm)[side]
        ref = M.at[zz] if whole else M.at[zz, side]
        rcopy(ref, ref, ms, mx.at[side, hop - 1], dev).start()

    def mwait(zz, side, hop, whole):
        dev = (zp, zm)[side]
        ref = M.at[zz] if whole else M.at[zz, side]
        rcopy(ref, ref, ms, mx.at[side, hop - 1], dev).wait_recv()

    def away(hop, side):
        return (z + 8 - hop) % 8 if side == 0 else (z + hop) % 8

    def ready(i):
        pltpu.make_async_copy(Z.at[i, z, mine], Z.at[i, z, mine], lsem.at[i]).wait()
        rcopy(Z.at[i, z, his], Z.at[i, z, his], psem, prx.at[i], mate).wait_recv()

    def z0(i):
        for side in range(2):
            zsend(i, z, side, 1, True)

    def own(i):
        ready(i)
        process((i, 0, z))

    def zhop(i, hop):
        for side in range(2):
            block = away(hop, side)

            @pl.when(i == 0)
            def _():
                mwait(block, side, hop, True)
                msend(block, side, hop + 1, hop < 3)

            zwait(i, block, side, hop, True)
            zsend(i, block, side, hop + 1, hop < 3)

    def z4(i):
        block = away(4, 1)

        @pl.when(i == 0)
        def _():
            for side in range(2):
                mwait(block, side, 4, False)

        for side in range(2):
            zwait(i, block, side, 4, False)

    def both_sides(i, hop):
        process((i, 2 * hop - 1, away(hop, 0)), (i, 2 * hop, away(hop, 1)))

    def arrive(ch, w):
        lo, hi = ((0, 5), (5, 7), (7, 8))[w]
        for k in range(3):
            ref = R.at[ch, lo:hi, :, 0]
            rcopy(ref, ref, xs, rx.at[ch, k, w], (xp, xo, xm)[k]).wait_recv()

    def turn(ch, lo, hi):
        @pl.loop(lo, hi)
        def _(b):
            cols = pl.ds(pl.multiple_of(b * KB, KB), KB)
            RT[:, cols] = R[ch, b].reshape(KB, WIDE).T

    def partial(lo, hi, cols):
        right = HB[lo:hi, :, :, :, cols].reshape((hi - lo) * KB, 256)
        return jnp.dot(RT[:, lo * KB:hi * KB], right, preferred_element_type=F32)

    def column_tiles(body):
        @pl.loop(0, 7)
        def _(n):
            body(pl.ds(pl.multiple_of(n * 256, 256), 256))

    def multiply_first(ch):
        arrive(ch, 0)
        turn(ch, 0, 5)

        @column_tiles
        def _(cols):
            ACC[:, cols] = partial(0, 5, cols)

    def multiply_rest(ch):
        arrive(ch, 1)
        arrive(ch, 2)
        turn(ch, 5, 8)

        @column_tiles
        def _(cols):
            ACC[:, cols] += partial(5, 8, cols)

    def ywait(ch, half):
        ref = YV.at[ch, half]
        rcopy(ref, ref, ys, yx.at[ch, half], (yp, ym)[half]).wait_recv()

    def reduce_send(ch):
        for half in range(2):
            @pl.when(ch == half + 1)
            def _():
                ywait(0, half)

                @pl.loop(0, 7)
                def _(n):
                    cols = pl.ds(pl.multiple_of(n * 256, 256), 256)
                    ACC[half * HALF:(half + 1) * HALF, cols] += YV[0, half, :, cols].astype(F32)

            @pl.loop(0, 7)
            def _(n):
                cols = pl.ds(pl.multiple_of(n * 256, 256), 256)
                YS[ch, half, :, cols] = ACC[half * HALF:(half + 1) * HALF, cols].astype(BF)

            rcopy(YS.at[ch, half], YV.at[ch, half], ys, yx.at[ch, half], (yp, ym)[half]).start()

    def count_send(step):
        dev = (bx1, bx2, by1, by2)[step]
        rcopy(CN.at[0, step], CN.at[1, step], cs, cx.at[step], dev).start()

    def count_wait(step):
        dev = (bx1, bx2, by1, by2)[step]
        rcopy(CN.at[1, step], CN.at[1, step], cs, cx.at[step], dev).wait_recv()
        return CN[0, step] + CN[1, step]

    rcopy(M.at[z, oc], M.at[z, oc], mps, mrx, mate).wait_recv()
    for side in range(2):
        msend(z, side, 1, True)

    ready(0)

    @pl.loop(0, 6)
    def _(q):
        one = jnp.minimum(jnp.maximum(q - 1, 0), 3)
        two = jnp.maximum(q - 2, 0)
        now = jnp.minimum(q, 3)
        young = q < 4
        middle = (q >= 1) & (q < 5)
        old = q >= 2
        done = (q >= 2) & (q < 5)

        pl.when(old)(lambda: z4(two))
        pl.when(middle)(lambda: zhop(one, 2))
        pl.when(young)(lambda: z0(now))

        @pl.when(q == 0)
        def _():
            process((0, 0, z))
            own(1)

        pl.when(old)(lambda: process((two, 7, away(4, 1))))
        pl.when(middle)(lambda: both_sides(one, 2))

        @pl.when(q == 2)
        def _():
            total = jnp.zeros((EXPERTS, TOK), F32)
            for zz in range(8):
                for cc in range(2):
                    total += jnp.where(M[zz, cc, 0:8, :] >= 0.0, 1.0, 0.0)
            CN[0, 0] = total
            count_send(0)
            pltpu.make_async_copy(HB.at[:, c], HB.at[:, c], hsem).wait()
            rcopy(HB.at[:, oc], HB.at[:, oc], hps, hrx, mate).wait_recv()

        for step in range(3):
            @pl.when(q == step + 3)
            def _():
                CN[0, step + 1] = count_wait(step)
                count_send(step + 1)

        pl.when(done)(lambda: multiply_first(two))
        pl.when(middle)(lambda: zhop(one, 3))
        pl.when(young)(lambda: zhop(now, 1))
        pl.when(middle)(lambda: both_sides(one, 3))
        pl.when(young)(lambda: both_sides(now, 1))
        pl.when(q < 2)(lambda: own(jnp.minimum(q + 2, 3)))

        @pl.when(done)
        def _():
            multiply_rest(two)
            reduce_send(two)

    multiply_first(3)
    total = count_wait(3)
    picked = jnp.where(er == 2 * x + h, total, 0.0)
    count = jnp.sum(jnp.sum(picked, axis=1, keepdims=True), axis=0, keepdims=True)
    factor = lax.rsqrt(1.0 + count)
    arrive(3, 1)
    turn(3, 5, 7)
    for ch in (1, 2):
        for half in range(2):
            ywait(ch, half)

    @column_tiles
    def _(cols):
        ACC[:, cols] += partial(5, 7, cols)
        for part in range(2):
            rows = slice(part * HALF, (part + 1) * HALF)
            ACC[rows, cols] += YV[part + 1, 0, :, cols].astype(F32) + YV[
                part + 1, 1, :, cols
            ].astype(F32)

    arrive(3, 2)
    turn(3, 7, 8)

    @column_tiles
    def _(cols):
        out_ref[:, cols] = (ACC[:, cols] + partial(7, 8, cols)) * factor

    rcopy(M.at[z, c], M.at[z, c], mps, mrx, mate).wait_send()
    sent = Z.at[:, 0, pl.ds(0, TOK)]
    rcopy(sent, sent, psem, prx.at[0], mate).wait_send()
    rcopy(HB.at[:, c], HB.at[:, c], hps, hrx, mate).wait_send()
    sent = M.at[pl.ds(0, 7)]
    rcopy(sent, sent, ms, mx.at[0, 0], zp).wait_send()
    sent = Z.at[:, pl.ds(0, 7)]
    rcopy(sent, sent, zs, zx.at[0, 0, 0], zp).wait_send()
    rcopy(S, S, xs, rx.at[0, 0, 0], xp).wait_send()
    rcopy(YS, YS, ys, yx.at[0, 0], yp).wait_send()
    rcopy(CN.at[0], CN.at[0], cs, cx.at[0], bx1).wait_send()


def on_device(d_out, routes, combine, live_tokens, hidden):
    dma = pltpu.SemaphoreType.DMA
    any_spec = pl.BlockSpec(memory_space=pl.ANY)
    vmem = pl.BlockSpec(memory_space=pltpu.VMEM)
    return pl.pallas_call(
        kernel,
        out_shape=jax.ShapeDtypeStruct((WIDE, 1792), F32),
        in_specs=[any_spec, vmem, vmem, vmem, any_spec],
        out_specs=vmem,
        scratch_shapes=[
            pltpu.VMEM((CHUNKS, 8, 2 * TOK, WIDE), BF),
            pltpu.VMEM((CHUNKS, 8, 2, 4, CAP, WIDE), BF),
            pltpu.VMEM((CHUNKS, 8, 3, 2, CAP, WIDE), BF),
            pltpu.VMEM((8, 2, 4, CAP, 1792), BF),
            pltpu.VMEM((8, 2, 4 * CAP, TOK), BF),
            pltpu.VMEM((8, 2, 4 * CAP, TOK), F32),
            pltpu.VMEM((8, 2, 16, TOK), F32),
            pltpu.VMEM((2, 4, EXPERTS, TOK), F32),
            pltpu.VMEM((WIDE, 2 * 1536), BF),
            pltpu.VMEM((WIDE, 1792), F32),
            pltpu.VMEM((3, 2, HALF, 1792), BF),
            pltpu.VMEM((3, 2, HALF, 1792), BF),
            dma((CHUNKS,)), dma, dma((CHUNKS,)), dma, dma, dma, dma, dma,
            dma, dma((CHUNKS, 2, 4)), dma, dma((2, 4)),
            dma, dma((CHUNKS, 3, 3)),
            dma, dma((3, 2)), dma, dma((4,)),
        ],
        compiler_params=pltpu.CompilerParams(
            collective_id=0, has_side_effects=True, vmem_limit_bytes=64000000
        ),
    )(d_out, routes.T, combine.T, live_tokens.reshape(1, 1), hidden.reshape(4, 8, CAP, 1792))


def solution(mesh):
    both = P(("grp", "ep"), None)
    return jax.shard_map(
        on_device, mesh=mesh,
        in_specs=(both, both, both, P(("grp", "ep")), P("grp", "ep")),
        out_specs=P("grp", "ep"), check_vma=False,
    )
```

time: 105 us -> 95.2 us (0.907)
  Pallas kernels: 102 us -> 91.5 us
    pallas_call x1, Pallas kernels: 102 us -> 91.5 us  [on_device(): pl.pallas_call(kernel, out_shape=jax.ShapeDtypeStruct((WIDE, 1792), F32),...]
where the time goes in v2:
time: 95.2 us; the launch traced here: 95.1 us
  Pallas kernels  91.5 us (96%)
  local copies, waits for them, and re-layouts  2.85 us (3%)
    pallas_call x1, Pallas kernels, on_device(): pl.pallas_call(kernel, out_shape=jax.ShapeDtypeStruct((WIDE, 1792), F32),...  91.5 us
    unnamed x1, local copies, waits for them, and re-layouts  2.85 us

profile of v2, /device:TPU:2, one launch (start us, length us, event | category | flops | bytes accessed | tf_op | source)
XLA Modules:
  0.0 95.1 jit_solution(13097340937512409613)
XLA Ops:
  0.7 91.5 %shard_map.55 = f32[256,1792]{1,0:T(8,128)} custom-call(bf16[128,2048]{1,0:T(8,128)(2,1)} %d_ref.1, s32[2,128]{1,0:T(2,128)} %bitcast.6, f32[2,128]{1,0:T(2,128)} %bitcast.7, s32[1,1]{1,0:T(1,128)} %bitcast.4.live_ref, bf16[4,8,48,1792]{3,2,1,0:T(8,128)(2,1)} %bitcast.5), custom_call_target="tpu_custom_call" | custom-call | tf_op jit(solution)/shard_map/pallas_call | solution.py:382
  92.2 2.8 %copy.8 = f32[256,1792]{1,0:T(8,128)} copy(f32[256,1792]{1,0:T(8,128)} %shard_map.55) | data formatting | bytes 3670016

commit v3 on v2

--- a/solution.py
+++ b/solution.py
@@ -304,6 +304,7 @@
             own(1)
 
         pl.when(old)(lambda: process((two, 7, away(4, 1))))
+        pl.when(q == 4)(lambda: both_sides(3, 1))
         pl.when(middle)(lambda: both_sides(one, 2))
 
         @pl.when(q == 2)
@@ -327,8 +328,17 @@
         pl.when(middle)(lambda: zhop(one, 3))
         pl.when(young)(lambda: zhop(now, 1))
         pl.when(middle)(lambda: both_sides(one, 3))
-        pl.when(young)(lambda: both_sides(now, 1))
-        pl.when(q < 2)(lambda: own(jnp.minimum(q + 2, 3)))
+        pl.when(q < 3)(lambda: both_sides(now, 1))
+
+        @pl.when(q == 0)
+        def _():
+            own(2)
+            ready(3)
+
+        @pl.when(q == 4)
+        def _():
+            process((3, 0, z))
+
 
         @pl.when(done)
         def _():
@@ -403,7 +413,7 @@
             dma, dma((3, 2)), dma, dma((4,)),
         ],
         compiler_params=pltpu.CompilerParams(
-            collective_id=0, has_side_effects=True, vmem_limit_bytes=64000000
+            collective_id=0, has_side_effects=True, vmem_limit_bytes=54000000
         ),
     )(d_out, routes.T, combine.T, live_tokens.reshape(1, 1), hidden.reshape(4, 8, CAP, 1792))
 

time: 95.2 us -> 93.4 us (0.981)
  Pallas kernels: 91.5 us -> 88.8 us
    pallas_call x1, Pallas kernels: 91.5 us -> 88.8 us  [on_device(): pl.pallas_call(kernel, out_shape=jax.ShapeDtypeStruct((WIDE, 1792), F32),...]
    unnamed x1 -> x7, local copies, waits for them, and re-layouts: 2.85 us -> 3.62 us
where the time goes in v3:
time: 93.4 us; the launch traced here: 93.1 us
  Pallas kernels  88.8 us (95%)
  local copies, waits for them, and re-layouts  3.62 us (4%)
    pallas_call x1, Pallas kernels, on_device(): pl.pallas_call(kernel, out_shape=jax.ShapeDtypeStruct((WIDE, 1792), F32),...  88.8 us
    unnamed x7, local copies, waits for them, and re-layouts  3.62 us

profile of v3, /device:TPU:2, one launch (start us, length us, event | category | flops | bytes accessed | tf_op | source)
XLA Modules:
  0.0 93.1 jit_solution(12956323864975348950)
XLA Ops:
  0.7 0.0 copy-start
  0.7 1.0 %copy-done = bf16[128,2048]{1,0:T(8,128)(2,1)S(1)} copy-done((bf16[128,2048]{1,0:T(8,128)(2,1)S(1)}, bf16[128,2048]{1,0:T(8,128)(2,1)}, u32[]{:S(2)}) %copy-start) | copy-done | bytes 524312
  1.7 0.0 copy-start.1
  1.7 0.7 copy-done.1
  2.4 0.0 copy-start.2
  2.4 0.7 copy-done.2
  3.1 88.8 %shard_map.55 = f32[256,1792]{1,0:T(8,128)S(1)} custom-call(bf16[128,2048]{1,0:T(8,128)(2,1)S(1)} %copy-done, s32[2,128]{1,0:T(2,128)S(1)} %bitcast.5, f32[2,128]{1,0:T(2,128)S(1)} %bitcast.6, s32[1,1]{1,0:T(1,128)} %bitcast.4.live_ref, bf16[4,8,48,1792]{3,2,1,0:T(8,128)(2,1)} %bitcast.7), custom_call_target="tpu_custom_call" | custom-call | tf_op jit(solution)/shard_map/pallas_call | solution.py:392
  91.9 1.2 %copy.8 = f32[256,1792]{1,0:T(8,128)} copy(f32[256,1792]{1,0:T(8,128)S(1)} %shard_map.55) | data formatting | bytes 3670016
Async XLA Ops:
  0.7 1.0 %copy-start = (bf16[128,2048]{1,0:T(8,128)(2,1)S(1)}, bf16[128,2048]{1,0:T(8,128)(2,1)}, u32[]{:S(2)}) copy-start(bf16[128,2048]{1,0:T(8,128)(2,1)} %d_ref.1) | copy-start | bytes 1572868
  1.7 0.7 copy-start.1
  2.4 0.7 copy-start.2

commit v4 on v2

--- a/solution.py
+++ b/solution.py
@@ -13,6 +13,19 @@
 CHUNKS = 4
 WIDE = 256
 HALF = 128
+PLAN = (
+    "z00", "p00", "r1", "p10", "r3",
+    "z01", "p01", "r2", "p20",
+    "z02", "z10", "p02",
+    "z03", "z11", "p03", "p11",
+    "z04", "z12", "z20", "p04", "p12", "c0", "h", "f0",
+    "z13", "z21", "p13", "p21", "l0",
+    "z14", "z22", "z30", "p14", "p22", "c1", "f1",
+    "z23", "z31", "p23", "p30", "c2", "l1",
+    "z24", "z32", "p24", "p31", "p32", "c3", "f2",
+    "z33", "p33", "l2",
+    "z34", "p34",
+)
 KB = 8 * CAP
 BF = jnp.bfloat16
 F32 = jnp.float32
@@ -130,8 +143,7 @@
 
     def process(*units):
         for i, b, zz in units:
-            @pl.when(i == 0)
-            def _():
+            if i == 0:
                 build_p(b, zz)
 
         for i, b, zz in units:
@@ -187,8 +199,7 @@
         for side in range(2):
             block = away(hop, side)
 
-            @pl.when(i == 0)
-            def _():
+            if i == 0:
                 mwait(block, side, hop, True)
                 msend(block, side, hop + 1, hop < 3)
 
@@ -198,8 +209,7 @@
     def z4(i):
         block = away(4, 1)
 
-        @pl.when(i == 0)
-        def _():
+        if i == 0:
             for side in range(2):
                 mwait(block, side, 4, False)
 
@@ -284,56 +294,48 @@
 
     ready(0)
 
-    @pl.loop(0, 6)
-    def _(q):
-        one = jnp.minimum(jnp.maximum(q - 1, 0), 3)
-        two = jnp.maximum(q - 2, 0)
-        now = jnp.minimum(q, 3)
-        young = q < 4
-        middle = (q >= 1) & (q < 5)
-        old = q >= 2
-        done = (q >= 2) & (q < 5)
-
-        pl.when(old)(lambda: z4(two))
-        pl.when(middle)(lambda: zhop(one, 2))
-        pl.when(young)(lambda: z0(now))
-
-        @pl.when(q == 0)
-        def _():
-            process((0, 0, z))
-            own(1)
-
-        pl.when(old)(lambda: process((two, 7, away(4, 1))))
-        pl.when(middle)(lambda: both_sides(one, 2))
-
-        @pl.when(q == 2)
-        def _():
+
+    def blocks(i, hop):
+        if hop == 0:
+            process((i, 0, z))
+        elif hop == 4:
+            process((i, 7, away(4, 1)))
+        else:
+            both_sides(i, hop)
+
+    def along_z(i, hop):
+        if hop == 0:
+            z0(i)
+        elif hop == 4:
+            z4(i)
+        else:
+            zhop(i, hop)
+
+    def count_step(k):
+        if k == 0:
             total = jnp.zeros((EXPERTS, TOK), F32)
             for zz in range(8):
                 for cc in range(2):
                     total += jnp.where(M[zz, cc, 0:8, :] >= 0.0, 1.0, 0.0)
             CN[0, 0] = total
-            count_send(0)
-            pltpu.make_async_copy(HB.at[:, c], HB.at[:, c], hsem).wait()
-            rcopy(HB.at[:, oc], HB.at[:, oc], hps, hrx, mate).wait_recv()
-
-        for step in range(3):
-            @pl.when(q == step + 3)
-            def _():
-                CN[0, step + 1] = count_wait(step)
-                count_send(step + 1)
-
-        pl.when(done)(lambda: multiply_first(two))
-        pl.when(middle)(lambda: zhop(one, 3))
-        pl.when(young)(lambda: zhop(now, 1))
-        pl.when(middle)(lambda: both_sides(one, 3))
-        pl.when(young)(lambda: both_sides(now, 1))
-        pl.when(q < 2)(lambda: own(jnp.minimum(q + 2, 3)))
-
-        @pl.when(done)
-        def _():
-            multiply_rest(two)
-            reduce_send(two)
+        else:
+            CN[0, k] = count_wait(k - 1)
+        count_send(k)
+
+    def hidden_here():
+        pltpu.make_async_copy(HB.at[:, c], HB.at[:, c], hsem).wait()
+        rcopy(HB.at[:, oc], HB.at[:, oc], hps, hrx, mate).wait_recv()
+
+    def multiply_last(ch):
+        multiply_rest(ch)
+        reduce_send(ch)
+
+    acts = dict(
+        r=ready, z=along_z, p=blocks, c=count_step, h=hidden_here, f=multiply_first,
+        l=multiply_last,
+    )
+    for step in PLAN:
+        acts[step[0]](*map(int, step[1:]))
 
     multiply_first(3)
     total = count_wait(3)
@@ -403,7 +405,7 @@
             dma, dma((3, 2)), dma, dma((4,)),
         ],
         compiler_params=pltpu.CompilerParams(
-            collective_id=0, has_side_effects=True, vmem_limit_bytes=64000000
+            collective_id=0, has_side_effects=True, vmem_limit_bytes=54000000
         ),
     )(d_out, routes.T, combine.T, live_tokens.reshape(1, 1), hidden.reshape(4, 8, CAP, 1792))
 

time: 95.2 us -> 90.6 us (0.952)
  Pallas kernels: 91.5 us -> 85.9 us
    pallas_call x1, Pallas kernels: 91.5 us -> 85.9 us  [on_device(): pl.pallas_call(kernel, out_shape=jax.ShapeDtypeStruct((WIDE, 1792), F32),...]
    unnamed x1 -> x7, local copies, waits for them, and re-layouts: 2.85 us -> 3.62 us
where the time goes in v4:
time: 90.6 us; the launch traced here: 90.2 us
  Pallas kernels  85.9 us (95%)
  local copies, waits for them, and re-layouts  3.62 us (4%)
    pallas_call x1, Pallas kernels, on_device(): pl.pallas_call(kernel, out_shape=jax.ShapeDtypeStruct((WIDE, 1792), F32),...  85.9 us
    unnamed x7, local copies, waits for them, and re-layouts  3.62 us

profile of v4, /device:TPU:2, one launch (start us, length us, event | category | flops | bytes accessed | tf_op | source)
XLA Modules:
  0.0 90.2 jit_solution(9223019933988327868)
XLA Ops:
  0.7 0.0 copy-start
  0.7 1.0 %copy-done = bf16[128,2048]{1,0:T(8,128)(2,1)S(1)} copy-done((bf16[128,2048]{1,0:T(8,128)(2,1)S(1)}, bf16[128,2048]{1,0:T(8,128)(2,1)}, u32[]{:S(2)}) %copy-start) | copy-done | bytes 524312
  1.7 0.0 copy-start.1
  1.7 0.7 copy-done.1
  2.4 0.0 copy-start.2
  2.4 0.7 copy-done.2
  3.1 85.9 %shard_map.55 = f32[256,1792]{1,0:T(8,128)S(1)} custom-call(bf16[128,2048]{1,0:T(8,128)(2,1)S(1)} %copy-done, s32[2,128]{1,0:T(2,128)S(1)} %bitcast.5, f32[2,128]{1,0:T(2,128)S(1)} %bitcast.6, s32[1,1]{1,0:T(1,128)} %bitcast.4.live_ref, bf16[4,8,48,1792]{3,2,1,0:T(8,128)(2,1)} %bitcast.7), custom_call_target="tpu_custom_call" | custom-call | tf_op jit(solution)/shard_map/pallas_call | solution.py:384
  88.9 1.2 %copy.8 = f32[256,1792]{1,0:T(8,128)} copy(f32[256,1792]{1,0:T(8,128)S(1)} %shard_map.55) | data formatting | bytes 3670016
Async XLA Ops:
  0.7 1.0 %copy-start = (bf16[128,2048]{1,0:T(8,128)(2,1)S(1)}, bf16[128,2048]{1,0:T(8,128)(2,1)}, u32[]{:S(2)}) copy-start(bf16[128,2048]{1,0:T(8,128)(2,1)} %d_ref.1) | copy-start | bytes 1572868
  1.7 0.7 copy-start.1
  2.4 0.7 copy-start.2

commit v5 on v4

--- a/solution.py
+++ b/solution.py
@@ -344,25 +344,27 @@
     factor = lax.rsqrt(1.0 + count)
     arrive(3, 1)
     turn(3, 5, 7)
-    for ch in (1, 2):
-        for half in range(2):
-            ywait(ch, half)
+    for half in range(2):
+        ywait(1, half)
+
+    def groups(part, cols):
+        return YV[part + 1, 0, :, cols].astype(F32) + YV[part + 1, 1, :, cols].astype(F32)
 
     @column_tiles
     def _(cols):
         ACC[:, cols] += partial(5, 7, cols)
-        for part in range(2):
-            rows = slice(part * HALF, (part + 1) * HALF)
-            ACC[rows, cols] += YV[part + 1, 0, :, cols].astype(F32) + YV[
-                part + 1, 1, :, cols
-            ].astype(F32)
+        ACC[:HALF, cols] += groups(0, cols)
 
     arrive(3, 2)
     turn(3, 7, 8)
+    for half in range(2):
+        ywait(2, half)
 
     @column_tiles
     def _(cols):
-        out_ref[:, cols] = (ACC[:, cols] + partial(7, 8, cols)) * factor
+        last = ACC[:, cols] + partial(7, 8, cols)
+        out_ref[:HALF, cols] = last[:HALF] * factor
+        out_ref[HALF:, cols] = (last[HALF:] + groups(1, cols)) * factor
 
     rcopy(M.at[z, c], M.at[z, c], mps, mrx, mate).wait_send()
     sent = Z.at[:, 0, pl.ds(0, TOK)]

time: 90.6 us -> 90.3 us (level)
  no operation moved by 1% of the time
where the time goes in v5:
time: 90.3 us; the launch traced here: 90.1 us
  Pallas kernels  85.8 us (95%)
  local copies, waits for them, and re-layouts  3.62 us (4%)
    pallas_call x1, Pallas kernels, on_device(): pl.pallas_call(kernel, out_shape=jax.ShapeDtypeStruct((WIDE, 1792), F32),...  85.8 us
    unnamed x7, local copies, waits for them, and re-layouts  3.62 us

profile of v5, /device:TPU:2, one launch (start us, length us, event | category | flops | bytes accessed | tf_op | source)
XLA Modules:
  0.0 90.1 jit_solution(2498639415834446887)
XLA Ops:
  0.7 0.0 copy-start
  0.7 1.0 %copy-done = bf16[128,2048]{1,0:T(8,128)(2,1)S(1)} copy-done((bf16[128,2048]{1,0:T(8,128)(2,1)S(1)}, bf16[128,2048]{1,0:T(8,128)(2,1)}, u32[]{:S(2)}) %copy-start) | copy-done | bytes 524312
  1.7 0.0 copy-start.1
  1.7 0.7 copy-done.1
  2.4 0.0 copy-start.2
  2.4 0.7 copy-done.2
  3.1 85.8 %shard_map.55 = f32[256,1792]{1,0:T(8,128)S(1)} custom-call(bf16[128,2048]{1,0:T(8,128)(2,1)S(1)} %copy-done, s32[2,128]{1,0:T(2,128)S(1)} %bitcast.5, f32[2,128]{1,0:T(2,128)S(1)} %bitcast.6, s32[1,1]{1,0:T(1,128)} %bitcast.4.live_ref, bf16[4,8,48,1792]{3,2,1,0:T(8,128)(2,1)} %bitcast.7), custom_call_target="tpu_custom_call" | custom-call | tf_op jit(solution)/shard_map/pallas_call | solution.py:386
  88.9 1.2 %copy.8 = f32[256,1792]{1,0:T(8,128)} copy(f32[256,1792]{1,0:T(8,128)S(1)} %shard_map.55) | data formatting | bytes 3670016
Async XLA Ops:
  0.7 1.0 %copy-start = (bf16[128,2048]{1,0:T(8,128)(2,1)S(1)}, bf16[128,2048]{1,0:T(8,128)(2,1)}, u32[]{:S(2)}) copy-start(bf16[128,2048]{1,0:T(8,128)(2,1)} %d_ref.1) | copy-start | bytes 1572868
  1.7 0.7 copy-start.1
  2.4 0.7 copy-start.2

commit v6 on v5

--- a/solution.py
+++ b/solution.py
@@ -14,8 +14,8 @@
 WIDE = 256
 HALF = 128
 PLAN = (
-    "z00", "p00", "r1", "p10", "r3",
-    "z01", "p01", "r2", "p20",
+    "z00", "p00", "r1", "p10", "r2", "p20", "r3",
+    "z01", "p01",
     "z02", "z10", "p02",
     "z03", "z11", "p03", "p11",
     "z04", "z12", "z20", "p04", "p12", "c0", "h", "f0",

time: 90.3 us -> 90.3 us (level)
  no operation moved by 1% of the time
where the time goes in v6:
time: 90.3 us; the launch traced here: 90.1 us
  Pallas kernels  85.8 us (95%)
  local copies, waits for them, and re-layouts  3.62 us (4%)
    pallas_call x1, Pallas kernels, on_device(): pl.pallas_call(kernel, out_shape=jax.ShapeDtypeStruct((WIDE, 1792), F32),...  85.8 us
    unnamed x7, local copies, waits for them, and re-layouts  3.62 us

profile of v6, /device:TPU:2, one launch (start us, length us, event | category | flops | bytes accessed | tf_op | source)
XLA Modules:
  0.0 90.1 jit_solution(14543668695268429712)
XLA Ops:
  0.7 0.0 copy-start
  0.7 1.0 %copy-done = bf16[128,2048]{1,0:T(8,128)(2,1)S(1)} copy-done((bf16[128,2048]{1,0:T(8,128)(2,1)S(1)}, bf16[128,2048]{1,0:T(8,128)(2,1)}, u32[]{:S(2)}) %copy-start) | copy-done | bytes 524312
  1.7 0.0 copy-start.1
  1.7 0.7 copy-done.1
  2.4 0.0 copy-start.2
  2.4 0.7 copy-done.2
  3.1 85.8 %shard_map.55 = f32[256,1792]{1,0:T(8,128)S(1)} custom-call(bf16[128,2048]{1,0:T(8,128)(2,1)S(1)} %copy-done, s32[2,128]{1,0:T(2,128)S(1)} %bitcast.5, f32[2,128]{1,0:T(2,128)S(1)} %bitcast.6, s32[1,1]{1,0:T(1,128)} %bitcast.4.live_ref, bf16[4,8,48,1792]{3,2,1,0:T(8,128)(2,1)} %bitcast.7), custom_call_target="tpu_custom_call" | custom-call | tf_op jit(solution)/shard_map/pallas_call | solution.py:386
  88.9 1.2 %copy.8 = f32[256,1792]{1,0:T(8,128)} copy(f32[256,1792]{1,0:T(8,128)S(1)} %shard_map.55) | data formatting | bytes 3670016
Async XLA Ops:
  0.7 1.0 %copy-start = (bf16[128,2048]{1,0:T(8,128)(2,1)S(1)}, bf16[128,2048]{1,0:T(8,128)(2,1)}, u32[]{:S(2)}) copy-start(bf16[128,2048]{1,0:T(8,128)(2,1)} %d_ref.1) | copy-start | bytes 1572868
  1.7 0.7 copy-start.1
  2.4 0.7 copy-start.2
